TPU v7x, 512 devices: a 8x2x16 block of a 8x8x16 slice. The times are simulated.
512 devices in a mesh: groups: 2 (over y), seq: 128 (over z, x), tp: 2 (over core).
Axes of the slice: x: 8, y: 2, z: 16, core: 2. Of those that a mesh axis runs over, the one named last changes fastest.
The devices are a block of a 8x8x16 slice.
Arguments:
- stream: bfloat16 [2048, 6144], P(('groups', 'seq'), 'tp'), parts along dimension 0, may hold values from -6 to 6
- queries: bfloat16 [2048, 6144], P(('groups', 'seq'), 'tp'), parts along dimension 0, may hold values from -6 to 6
- key_rows: bfloat16 [2048, 1024], P(('groups', 'seq'), 'tp'), parts along dimension 0, may hold values from -6 to 6
- value_rows: bfloat16 [2048, 1024], P(('groups', 'seq'), 'tp'), parts along dimension 0, may hold values from -6 to 6
- routes: int32 [2048, 2], P(('groups', 'seq')), parts along dimension 0, may hold values from 0 to 3, all different within a row; in each aligned block of 8 rows (0 to 7, 8 to 15, ...) at most 4 rows name the same one
- seq_length: int32 [2], P('groups'), parts along dimension 0, may hold values from 256 to 1024
- norm_gain: float32 [6144], P('tp'), may hold values from 0.25 to 1.75
- router: float32 [6144, 4], P('tp'), may hold values from -0.078125 to 0.078125
- w_up: bfloat16 [6144, 32768], P('tp', 'seq'), may hold values from -0.078125 to 0.078125
- w_down: bfloat16 [32768, 6144], P('seq', 'tp'), may hold values from -0.0625 to 0.0625
- final_gain: float32 [6144], P('tp'), may hold values from 0.25 to 1.75
- value_weight: float32 [6144], P('tp'), may hold values from -0.078125 to 0.078125
- value_bias: float32 [1], replicated, may hold values from -3 to 3
Outputs:
- layer_out: bfloat16 [2048, 6144], P(('groups', 'seq'), 'tp'), parts along dimension 0
- values: float32 [2048], P(('groups', 'seq')), parts along dimension 0
There are 2 independent parts, one for each index of `groups`. A program takes and returns all parts, laid end to end along the dimension named above; an argument that names none is the same for every part. Nothing has to cross between parts.
Inputs may be any that keep to these rules, and one draw needn't show every extreme that they name: `routes`: each row names two different experts; among the rows on one device no expert is named more than 4 times, and some device's rows name some expert exactly 4 times.
All inputs are finite; a program needn't handle non-finite values.
Results may differ from a plain program's by a relative error of at most 0.01.
Values may be sent and summed in bfloat16 or wider, within the bound.
A program may use at most 64 MiB of HBM per device.

v0:
```python
import math
import jax
import jax.numpy as jnp
from jax import lax
from jax.sharding import Mesh
from jax.sharding import PartitionSpec as P

D = 6144
HD = 128
EXPERTS = 4
SEQ = ("seq_0", "seq_1")
GROUPS_SEQ = ("groups", "seq_0", "seq_1")
eps = 1e-05
masked = -1e30


def sent_together(arrays, axis, dim, along):
    both = jnp.concatenate(arrays, axis=along)
    result, at, done = (lax.all_gather(both, axis, axis=dim, tiled=True), 0, [])
    for a in arrays:
        done.append(lax.slice_in_dim(result, at, at + a.shape[along], axis=along))
        at += a.shape[along]
    return tuple(done)


def over_pieces(array, axis):
    pieces = lax.all_gather(array, axis)
    return pieces.sum(axis=0)


def from_everyone(array, axis):
    length = lax.axis_size(axis)
    return lax.all_to_all(
        jnp.broadcast_to(array[None], (length, *array.shape)), axis, 0, 0, tiled=True
    )


def of_everyone(array, axis):
    return from_everyone(array, axis).astype(jnp.float32).sum(axis=0)


def laid_out(pieces, dim):
    lengths = list(pieces.shape[1:])
    lengths[dim] *= pieces.shape[0]
    return jnp.moveaxis(pieces, 0, dim).reshape(lengths)


def stacked_from(array, axes, sequence):
    pieces = array
    for k in sequence:
        pieces = lax.all_gather(pieces, axes[k])
    done = sequence[::-1]
    back = [done.index(k) for k in range(len(axes))]
    pieces = pieces.transpose(*back, *range(len(axes), pieces.ndim))
    return pieces.reshape(-1, *array.shape)


def whole_of(array, axes, sequence, dim):
    return laid_out(stacked_from(array, axes, sequence), dim)


def on_device(
    stream,
    queries,
    key_rows,
    value_rows,
    routes,
    seq_length,
    norm_gain,
    router,
    w_up,
    w_down,
    final_gain,
    value_weight,
    value_bias,
):
    row_count = stream.shape[0]
    half_width = stream.shape[1]
    seq_devices = lax.axis_size(SEQ)
    owners = seq_devices // EXPERTS
    my_index = lax.axis_index(SEQ)
    seq_limit = seq_length[0]
    positions = my_index * row_count + jnp.arange(row_count, dtype=jnp.int32)
    kv_heads = key_rows.shape[1] // HD
    per_group = queries.shape[1] // HD // kv_heads
    grouped = queries.reshape(row_count, kv_heads, per_group, HD)
    inv_root = 1.0 / math.sqrt(HD)
    slot_cap = row_count // 2
    run_max = jnp.full((kv_heads, per_group, row_count), masked, jnp.float32)
    key_block, value_block = sent_together((key_rows, value_rows), SEQ, 0, 1)
    key_count = key_block.shape[0]
    scores = (
        jnp.einsum(
            "qkgd,ckd->kgqc",
            grouped,
            key_block.reshape(key_count, kv_heads, HD),
            preferred_element_type=jnp.float32,
        )
        * inv_root
    )
    key_pos = jnp.arange(key_count, dtype=jnp.int32)
    allowed = (key_pos[None, :] <= positions[:, None]) & (key_pos[None, :] < seq_limit)
    scores = jnp.where(allowed, scores, masked)
    new_max = jnp.maximum(run_max, jnp.max(scores, axis=-1))
    weights = jnp.where(allowed, jnp.exp(scores - new_max[..., None]), 0.0)
    new_sum = jnp.sum(weights, axis=-1)
    update = jnp.einsum(
        "kgqc,ckd->kgqd",
        weights.astype(jnp.bfloat16),
        value_block.reshape(key_count, kv_heads, HD),
        preferred_element_type=jnp.float32,
    )
    attended = (update / new_sum[..., None]).transpose(2, 0, 1, 3).reshape(row_count, half_width)
    hidden = stream.astype(jnp.float32) + attended
    gained = hidden * norm_gain
    squares = jnp.sum(hidden * hidden, axis=1)
    total_sq, raw_logits = (over_pieces(squares, "tp"), over_pieces(jnp.dot(gained, router), "tp"))
    norm_scale = lax.rsqrt(total_sq / D + eps)
    normed = gained * norm_scale[:, None]
    logits = raw_logits * norm_scale[:, None]
    normed_half = normed.astype(jnp.bfloat16)
    expert_ids = jnp.arange(EXPERTS, dtype=jnp.int32)
    chosen = (routes[:, :, None] == expert_ids).astype(jnp.float32)
    picked = jnp.sum(chosen * logits[:, None, :], axis=2)
    gates = jax.nn.sigmoid(picked - picked[:, ::-1])
    flat_hits = chosen.reshape(row_count * 2, EXPERTS)
    earlier = jnp.cumsum(flat_hits, axis=0) - flat_hits
    slot_index = jnp.sum(earlier * flat_hits, axis=1).astype(jnp.int32)
    target = routes.reshape(row_count * 2) * slot_cap + slot_index
    placing = (target[:, None] == jnp.arange(EXPERTS * slot_cap, dtype=jnp.int32)[None, :]).astype(
        jnp.bfloat16
    )
    every_row = lax.all_gather(normed_half, SEQ, axis=0, tiled=True)
    every_route = whole_of(routes, SEQ, (0, 1), 0)
    my_expert = my_index // owners
    row_hits = jnp.sum((every_route == my_expert).astype(jnp.int32), axis=1).reshape(
        seq_devices, row_count
    )
    ranks = jnp.cumsum(row_hits, axis=1) - row_hits
    selector = (
        (ranks[:, :, None] == jnp.arange(slot_cap, dtype=jnp.int32)[None, None, :])
        & (row_hits[:, :, None] > 0)
    ).astype(jnp.bfloat16)
    arrived = jnp.einsum(
        "src,srd->scd",
        selector,
        every_row.reshape(seq_devices, row_count, half_width),
        preferred_element_type=jnp.float32,
    ).astype(jnp.bfloat16)
    lead = arrived.shape[0]
    items = arrived.shape[1]
    flat_rows = arrived.reshape(lead * items, half_width)
    up_part = jnp.dot(flat_rows, w_up, preferred_element_type=jnp.float32)
    up_total = of_everyone(up_part.astype(jnp.bfloat16), "tp").astype(jnp.float32)
    active = jax.nn.silu(up_total).astype(jnp.bfloat16)
    down_part = jnp.dot(active, w_down, preferred_element_type=jnp.float32).astype(jnp.bfloat16)
    partial_out = down_part.reshape(lead, items, half_width)
    returned = lax.all_to_all(partial_out, SEQ, split_axis=0, concat_axis=0, tiled=True)
    summed = jnp.sum(
        returned.reshape(EXPERTS, owners, slot_cap, half_width), axis=1, dtype=jnp.float32
    ).reshape(EXPERTS * slot_cap, half_width)
    fetched = jnp.dot(placing.astype(jnp.float32), summed)
    mixed = jnp.sum(fetched.reshape(row_count, 2, half_width) * gates[:, :, None], axis=1)
    final = hidden + mixed
    sq_part = jnp.sum(final * final, axis=1)
    dot_part = jnp.sum(final * (final_gain * value_weight), axis=1)
    sq_total, dot_total = (over_pieces(sq_part, "tp"), over_pieces(dot_part, "tp"))
    estimate = dot_total * lax.rsqrt(sq_total / D + eps) + value_bias[0]
    estimate = jnp.where(positions < seq_limit, estimate, 0.0)
    return (final.astype(jnp.bfloat16), estimate)


def solution(mesh):
    finer = Mesh(
        mesh.devices.reshape(mesh.shape["groups"], 16, 8, mesh.shape["tp"]),
        ("groups", "seq_0", "seq_1", "tp"),
    )
    placed = (
        P(GROUPS_SEQ, "tp"),
        P(GROUPS_SEQ, "tp"),
        P(GROUPS_SEQ, "tp"),
        P(GROUPS_SEQ, "tp"),
        P(GROUPS_SEQ, None),
        P("groups"),
        P("tp"),
        P("tp", None),
        P("tp", SEQ),
        P(SEQ, "tp"),
        P("tp"),
        P("tp"),
        P(),
    )
    return jax.shard_map(
        on_device,
        mesh=finer,
        in_specs=placed,
        out_specs=(P(GROUPS_SEQ, "tp"), P(GROUPS_SEQ)),
        check_vma=False,
    )
```

profile of v0, /device:TPU:65, one launch (start us, length us, event | category | flops | bytes accessed | tf_op | source)
XLA Modules:
  0.0 552.6 jit_solution(5043075534300548686)
XLA Ops:
  7.3 1.4 pad_maximum_fusion
  9.5 1.3 dynamic-slice
  11.5 169.5 %all-gather.11.cloned.1.call-done = bf16[1024,1024]{1,0:T(8,128)(2,1)} async-done(((bf16[8,1024]{1,0:T(8,128)(2,1)}), bf16[1024,1024]{1,0:T(8,128)(2,1)}) %all-gather.11.cloned.1.call-update) | async-done | bytes 2097168 | tf_op jit(solution)/shard_map/all_gather | solution.py:19
  181.0 2.7 fusion.32
  183.7 2.3 copy.70
  186.0 1.6 fusion.33
  187.6 1.3 copy.71
  189.2 1.7 fusion.8
  191.3 12.9 %all-reduce = f32[16]{0:T(128)S(1)} all-reduce(f32[16]{0:T(128)S(1)} %dynamic-update-slice), channel_id=4, replica_groups=mesh['groups'=2,'seq_0'=16,'seq_1'=8,'tp'=2] {'tp'}, use_global_device_ids=true, to_apply=%add | all-reduce | flops 16 | bytes 128
  205.1 20.9 %all-gather.6 = s32[16,8,2]{1,2,0:T(2,128)S(1)} all-gather(s32[1,8,2]{1,2,0:T(2,128)S(1)} %bitcast.63), channel_id=2, replica_groups=mesh['groups'=2,'seq_0'=16,'seq_1'=8,'tp'=2] {'seq_0'}, dimensions={0}, use_global_device_ids=true | all-gather | bytes 1088 | tf_op jit(solution)/shard_map/all_gather | solution.py:51
  226.0 19.8 %all-gather.1 = s32[128,8,2]{1,2,0:T(2,128)S(1)} all-gather(s32[16,8,2]{1,2,0:T(2,128)S(1)} %all-gather.6), channel_id=3, replica_groups=mesh['groups'=2,'seq_0'=16,'seq_1'=8,'tp'=2] {'seq_1'}, dimensions={0}, use_global_device_ids=true | all-gather | bytes 9216 | tf_op jit(solution)/shard_map/all_gather | solution.py:51
  246.4 96.1 %all-gather.13.cloned.1.call-done = bf16[1024,3072]{1,0:T(8,128)(2,1)} async-done(((bf16[8,3072]{1,0:T(8,128)(2,1)}), bf16[1024,3072]{1,0:T(8,128)(2,1)}) %all-gather.13.cloned.1.call-update) | async-done | bytes 6291472 | tf_op jit(solution)/shard_map/all_gather | solution.py:133
  342.5 6.3 %fusion.2 = bf16[128,4,3072]{2,1,0:T(4,128)(2,1)} fusion(bf16[1024,3072]{1,0:T(8,128)(2,1)} %all-gather.13.cloned.1.call-done, s32[128,8]{1,0:T(8,128)S(1)} %copy.60, pred[128,8]{1,0:T(8,128)(4,1)S(1)} %copy.61), kind=kOutput, calls=%fused_computation.3 | convolution fusion | flops 26746880 | bytes 9442304 | tf_op jit(solution)/shard_map/src,srd->scd/dot_general | solution.py:144
  348.8 5.9 %reshape.135 = bf16[512,3072]{1,0:T(8,128)(2,1)} reshape(bf16[128,4,3072]{2,1,0:T(4,128)(2,1)} %fusion.2) | data formatting | bytes 6291456 | tf_op jit(solution)/shard_map/reshape | solution.py:152
  354.7 3.3 convolution_convert_fusion.1
  358.1 11.9 %all_to_all.10 = bf16[2,512,256]{2,1,0:T(8,128)(2,1)S(1)} all-to-all(bf16[2,512,256]{2,1,0:T(8,128)(2,1)S(1)} %broadcast_in_dim.23), channel_id=1, replica_groups=mesh['groups'=2,'seq_0'=16,'seq_1'=8,'tp'=2] {'tp'}, dimensions={0} | all-to-all | bytes 1048576 | tf_op jit(solution)/shard_map/all_to_all | solution.py:33
  370.1 2.7 convolution_convert_fusion
  372.8 6.1 %reshape.136 = bf16[128,4,3072]{2,1,0:T(4,128)(2,1)} reshape(bf16[512,3072]{1,0:T(8,128)(2,1)} %convolution_convert_fusion) | data formatting | bytes 6291456 | tf_op jit(solution)/shard_map/reshape | solution.py:157
  378.9 17.0 %all-to-all-start.1 = ((bf16[128,4,3072]{2,1,0:T(4,128)(2,1)}), bf16[128,4,3072]{2,1,0:T(4,128)(2,1)}, u32[]{:S(2)}, u32[]{:S(2)}) async-start(bf16[128,4,3072]{2,1,0:T(4,128)(2,1)} %reshape.136), calls=%async_computation.1 | async-start | bytes 6291456 | tf_op jit(solution)/shard_map/all_to_all | solution.py:158
  397.4 2.2 all-gather.7
  399.6 132.8 %all-to-all-done.1 = bf16[128,4,3072]{2,1,0:T(4,128)(2,1)} async-done(((bf16[128,4,3072]{2,1,0:T(4,128)(2,1)}), bf16[128,4,3072]{2,1,0:T(4,128)(2,1)}, u32[]{:S(2)}, u32[]{:S(2)}) %all-to-all-start.1) | async-done | bytes 3145760 | tf_op jit(solution)/shard_map/all_to_all | solution.py:158
  532.5 3.2 convert_reduce_fusion
  535.9 0.8 multiply_reduce_fusion
  537.1 7.9 %all-reduce.3 = (f32[16]{0:T(128)S(1)}, f32[16]{0:T(128)S(1)}) all-reduce(f32[16]{0:T(128)S(1)} %dynamic-update-slice.1, f32[16]{0:T(128)S(1)} %dynamic-update-slice.2), channel_id=6, replica_groups=mesh['groups'=2,'seq_0'=16,'seq_1'=8,'tp'=2] {'tp'}, use_global_device_ids=true, to_apply=%add.1 | all-reduce | flops 32 | bytes 256
  (69 shorter events, 4.9 us)
Async XLA Ops:
  7.2 362.9 %copy-start = (bf16[256,3072]{1,0:T(8,128)(2,1)S(1)}, bf16[256,3072]{1,0:T(8,128)(2,1)}, u32[]{:S(2)}) copy-start(bf16[256,3072]{1,0:T(8,128)(2,1)} %param.22) | copy-start | bytes 4718596
  7.2 173.8 %all-gather.11.cloned.1.call-start = ((), (), s32[]{:S(2)}) async-start(), calls=%async_computation.2 | async-start | bytes 2113536 | tf_op jit(solution)/shard_map/all_gather | solution.py:19
  8.7 333.8 %all-gather.13.cloned.1.call-start = ((), (), s32[]{:S(2)}) async-start(), calls=%async_computation.3 | async-start | bytes 6340608 | tf_op jit(solution)/shard_map/all_gather | solution.py:133
  11.5 174.5 %copy-start.7 = (bf16[8,3072]{1,0:T(8,128)(2,1)S(1)}, bf16[8,3072]{1,0:T(8,128)(2,1)}, u32[]{:S(2)}) copy-start(bf16[8,3072]{1,0:T(8,128)(2,1)} %param.14) | copy-start | bytes 147460
  187.5 3.4 copy-start.1
  187.6 16.7 %copy-start.2 = (f32[3072]{0:T(1024)S(1)}, f32[3072]{0:T(1024)}, u32[]{:S(2)}) copy-start(f32[3072]{0:T(1024)} %param.19) | copy-start | bytes 36868
  187.6 17.5 %copy-start.6 = (s32[8,2]{0,1:T(2,128)S(1)}, s32[8,2]{0,1:T(2,128)}, u32[]{:S(2)}) copy-start(s32[8,2]{0,1:T(2,128)} %param.17) | copy-start | bytes 196
  378.9 18.3 %copy-start.4 = (f32[3072]{0:T(1024)S(1)}, f32[3072]{0:T(1024)}, u32[]{:S(2)}) copy-start(f32[3072]{0:T(1024)} %param.23) | copy-start | bytes 36868
  378.9 18.3 %copy-start.5 = (f32[3072]{0:T(1024)S(1)}, f32[3072]{0:T(1024)}, u32[]{:S(2)}) copy-start(f32[3072]{0:T(1024)} %param.24) | copy-start | bytes 36868
  378.9 18.3 %copy-start.3 = (f32[3072,4]{0,1:T(4,128)S(1)}, f32[3072,4]{0,1:T(4,128)}, u32[]{:S(2)}) copy-start(f32[3072,4]{0,1:T(4,128)} %param.20) | copy-start | bytes 147460
  378.9 153.6 %all-to-all-start.1 = ((bf16[128,4,3072]{2,1,0:T(4,128)(2,1)}), bf16[128,4,3072]{2,1,0:T(4,128)(2,1)}, u32[]{:S(2)}, u32[]{:S(2)}) async-start(bf16[128,4,3072]{2,1,0:T(4,128)(2,1)} %reshape.136), calls=%async_computation.1 | async-start | bytes 6291456 | tf_op jit(solution)/shard_map/all_to_all | solution.py:158
Sparse Core Ops, SparseCore 0:
  11.6 169.3 all-gather.10
  205.2 137.3 all-gather.12
where the time goes:
time: 553 us
  waiting for transfers between devices  399 us (72%)
  blocking collectives  75.5 us (14%)
  local copies, waits for them, and re-layouts  21.4 us (4%)
  starting transfers between devices  17.1 us (3%)
  between operations  16.3 us (3%)
  matrix products  15.9 us (3%)
  other arithmetic  7.87 us (1%)
    all_gather x1, waiting for transfers between devices, sent_together(): result, at, done = (lax.all_gather(both, axis, axis=dim, tiled=True), 0, [])  170 us
    all_to_all x1, waiting for transfers between devices, on_device(): lax.all_to_all(partial_out, SEQ, split_axis=0, concat_axis=0, tiled=True)  133 us
    all_gather x1, waiting for transfers between devices, on_device(): every_row = lax.all_gather(normed_half, SEQ, axis=0, tiled=True)  96.1 us
    all_gather x2, blocking collectives, stacked_from(): pieces = lax.all_gather(pieces, axes[k])  40.7 us
    unnamed x2, blocking collectives  20.7 us
    all_to_all x1, starting transfers between devices, on_device(): lax.all_to_all(partial_out, SEQ, split_axis=0, concat_axis=0, tiled=True)  17 us
    all_to_all x1, blocking collectives, from_everyone(): lax.all_to_all(jnp.broadcast_to(array[None], (length, *array.shape)), axi...  11.9 us
  transfers between devices with their start and end apart: 3, of which 3 were waited for; matrix products, arithmetic and copies ran while one was open for 1% of the time, Pallas kernels for 0%

commit v1 on v0

--- a/solution.py
+++ b/solution.py
@@ -130,7 +130,9 @@
     placing = (target[:, None] == jnp.arange(EXPERTS * slot_cap, dtype=jnp.int32)[None, :]).astype(
         jnp.bfloat16
     )
-    every_row = lax.all_gather(normed_half, SEQ, axis=0, tiled=True)
+    every_row = jnp.concatenate(
+        lax.all_to_all(jnp.stack([normed_half] * lax.axis_size(SEQ)), SEQ, 0, 0), axis=0
+    )
     every_route = whole_of(routes, SEQ, (0, 1), 0)
     my_expert = my_index // owners
     row_hits = jnp.sum((every_route == my_expert).astype(jnp.int32), axis=1).reshape(

time: 553 us -> 748 us (1.35)
  blocking collectives: 75.5 us -> 344 us
  waiting for transfers between devices: 399 us -> 303 us
  starting transfers between devices: 17.1 us -> 35.4 us
    all_gather x2, blocking collectives: 40.7 us -> 306 us  [stacked_from(): pieces = lax.all_gather(pieces, axes[k])]
    all_gather x1 -> x0, waiting for transfers between devices: 96.1 us -> none  [on_device(): every_row = lax.all_gather(normed_half, SEQ, axis=0, tiled=True)]
    all_to_all x0 -> x1, starting transfers between devices: none -> 17 us  [on_device(): lax.all_to_all(jnp.stack([normed_half] * lax.axis_size(SEQ)), SEQ, 0, 0)]
  transfers between devices with their start and end apart: 3 -> 3, of which waited for: 3 -> 2; matrix products, arithmetic and copies ran while one was open for 1% -> 0% of each run, Pallas kernels for 0% -> 0%
where the time goes in v1:
time: 748 us; the launch traced here: 747 us
  blocking collectives  344 us (46%)
  waiting for transfers between devices  303 us (41%)
  starting transfers between devices  35.4 us (5%)
  local copies, waits for them, and re-layouts  24.8 us (3%)
  between operations  16.3 us (2%)
  matrix products  15.9 us (2%)
    all_gather x2, blocking collectives, stacked_from(): pieces = lax.all_gather(pieces, axes[k])  306 us
    all_gather x1, waiting for transfers between devices, sent_together(): result, at, done = (lax.all_gather(both, axis, axis=dim, tiled=True), 0, [])  170 us
    all_to_all x1, waiting for transfers between devices, on_device(): lax.all_to_all(partial_out, SEQ, split_axis=0, concat_axis=0, tiled=True)  133 us
    unnamed x2, blocking collectives  20.8 us
    all_to_all x1, starting transfers between devices, on_device(): lax.all_to_all(partial_out, SEQ, split_axis=0, concat_axis=0, tiled=True)  18.4 us
    all_to_all x1, starting transfers between devices, on_device(): lax.all_to_all(jnp.stack([normed_half] * lax.axis_size(SEQ)), SEQ, 0, 0)  17 us
    all_to_all x1, blocking collectives, from_everyone(): lax.all_to_all(jnp.broadcast_to(array[None], (length, *array.shape)), axi...  15.9 us
  transfers between devices with their start and end apart: 3, of which 2 were waited for; matrix products, arithmetic and copies ran while one was open for 0% of the time, Pallas kernels for 0%

profile of v1, /device:TPU:65, one launch (start us, length us, event | category | flops | bytes accessed | tf_op | source)
XLA Modules:
  0.0 746.6 jit_solution(14815669479328756627)
XLA Ops:
  7.3 1.4 pad_maximum_fusion
  9.4 1.3 dynamic-slice
  11.4 169.6 %all-gather.10.cloned.1.call-done = bf16[1024,1024]{1,0:T(8,128)(2,1)} async-done(((bf16[8,1024]{1,0:T(8,128)(2,1)}), bf16[1024,1024]{1,0:T(8,128)(2,1)}) %all-gather.10.cloned.1.call-update) | async-done | bytes 2097168 | tf_op jit(solution)/shard_map/all_gather | solution.py:19
  181.0 2.7 fusion.27
  183.7 2.3 copy.70
  186.0 1.6 fusion.28
  187.6 1.3 copy.71
  189.2 1.7 fusion.3
  191.3 12.9 %all-reduce = f32[16]{0:T(128)S(1)} all-reduce(f32[16]{0:T(128)S(1)} %dynamic-update-slice), channel_id=4, replica_groups=mesh['groups'=2,'seq_0'=16,'seq_1'=8,'tp'=2] {'tp'}, use_global_device_ids=true, to_apply=%add | all-reduce | flops 16 | bytes 128
  204.4 3.4 stack.2
  207.8 17.0 %all-to-all-start = ((bf16[128,8,3072]{2,1,0:T(8,128)(2,1)}), bf16[128,8,3072]{2,1,0:T(8,128)(2,1)}, u32[]{:S(2)}, u32[]{:S(2)}) async-start(bf16[128,8,3072]{2,1,0:T(8,128)(2,1)} %stack.2), calls=%async_computation | async-start | bytes 12582912 | tf_op jit(solution)/shard_map/all_to_all | solution.py:134
  224.8 285.7 %all-gather.6 = s32[16,8,2]{1,2,0:T(2,128)S(1)} all-gather(s32[1,8,2]{1,2,0:T(2,128)S(1)} %bitcast.59), channel_id=2, replica_groups=mesh['groups'=2,'seq_0'=16,'seq_1'=8,'tp'=2] {'seq_0'}, dimensions={0}, use_global_device_ids=true | all-gather | bytes 1088 | tf_op jit(solution)/shard_map/all_gather | solution.py:51
  510.5 19.9 %all-gather.1 = s32[128,8,2]{1,2,0:T(2,128)S(1)} all-gather(s32[16,8,2]{1,2,0:T(2,128)S(1)} %all-gather.6), channel_id=3, replica_groups=mesh['groups'=2,'seq_0'=16,'seq_1'=8,'tp'=2] {'seq_1'}, dimensions={0}, use_global_device_ids=true | all-gather | bytes 9216 | tf_op jit(solution)/shard_map/all_gather | solution.py:51
  531.1 6.3 convolution_convert_fusion.1
  537.4 5.9 reshape.133
  543.2 3.3 convolution_convert_fusion.2
  546.6 15.9 %all_to_all.15 = bf16[2,512,256]{2,1,0:T(8,128)(2,1)S(1)} all-to-all(bf16[2,512,256]{2,1,0:T(8,128)(2,1)S(1)} %broadcast_in_dim.23), channel_id=1, replica_groups=mesh['groups'=2,'seq_0'=16,'seq_1'=8,'tp'=2] {'tp'}, dimensions={0} | all-to-all | bytes 1048576 | tf_op jit(solution)/shard_map/all_to_all | solution.py:33
  562.6 2.7 convolution_convert_fusion
  565.4 6.1 reshape.134
  571.5 18.4 %all-to-all-start.2 = ((bf16[128,4,3072]{2,1,0:T(4,128)(2,1)}), bf16[128,4,3072]{2,1,0:T(4,128)(2,1)}, u32[]{:S(2)}, u32[]{:S(2)}) async-start(bf16[128,4,3072]{2,1,0:T(4,128)(2,1)} %reshape.134), calls=%async_computation.2 | async-start | bytes 6291456 | tf_op jit(solution)/shard_map/all_to_all | solution.py:160
  591.4 2.1 all-gather.7
  593.5 132.9 %all-to-all-done.2 = bf16[128,4,3072]{2,1,0:T(4,128)(2,1)} async-done(((bf16[128,4,3072]{2,1,0:T(4,128)(2,1)}), bf16[128,4,3072]{2,1,0:T(4,128)(2,1)}, u32[]{:S(2)}, u32[]{:S(2)}) %all-to-all-start.2) | async-done | bytes 3145760 | tf_op jit(solution)/shard_map/all_to_all | solution.py:160
  726.4 3.2 convert_reduce_fusion
  731.1 7.9 %all-reduce.3 = (f32[16]{0:T(128)S(1)}, f32[16]{0:T(128)S(1)}) all-reduce(f32[16]{0:T(128)S(1)} %dynamic-update-slice.1, f32[16]{0:T(128)S(1)} %dynamic-update-slice.2), channel_id=6, replica_groups=mesh['groups'=2,'seq_0'=16,'seq_1'=8,'tp'=2] {'tp'}, use_global_device_ids=true, to_apply=%add.1 | all-reduce | flops 32 | bytes 256
  (69 shorter events, 4.9 us)
Async XLA Ops:
  7.2 555.5 %copy-start = (bf16[256,3072]{1,0:T(8,128)(2,1)S(1)}, bf16[256,3072]{1,0:T(8,128)(2,1)}, u32[]{:S(2)}) copy-start(bf16[256,3072]{1,0:T(8,128)(2,1)} %param.22) | copy-start | bytes 4718596
  7.2 173.8 %all-gather.10.cloned.1.call-start = ((), (), s32[]{:S(2)}) async-start(), calls=%async_computation.3 | async-start | bytes 2113536 | tf_op jit(solution)/shard_map/all_gather | solution.py:19
  11.4 174.5 %copy-start.7 = (bf16[8,3072]{1,0:T(8,128)(2,1)S(1)}, bf16[8,3072]{1,0:T(8,128)(2,1)}, u32[]{:S(2)}) copy-start(bf16[8,3072]{1,0:T(8,128)(2,1)} %param.14) | copy-start | bytes 147460
  187.5 3.4 copy-start.1
  187.6 16.7 %copy-start.2 = (f32[3072]{0:T(1024)S(1)}, f32[3072]{0:T(1024)}, u32[]{:S(2)}) copy-start(f32[3072]{0:T(1024)} %param.19) | copy-start | bytes 36868
  207.8 17.0 %copy-start.6 = (s32[8,2]{0,1:T(2,128)S(1)}, s32[8,2]{0,1:T(2,128)}, u32[]{:S(2)}) copy-start(s32[8,2]{0,1:T(2,128)} %param.17) | copy-start | bytes 196
  207.8 323.3 %all-to-all-start = ((bf16[128,8,3072]{2,1,0:T(8,128)(2,1)}), bf16[128,8,3072]{2,1,0:T(8,128)(2,1)}, u32[]{:S(2)}, u32[]{:S(2)}) async-start(bf16[128,8,3072]{2,1,0:T(8,128)(2,1)} %stack.2), calls=%async_computation | async-start | bytes 12582912 | tf_op jit(solution)/shard_map/all_to_all | solution.py:134
  571.5 19.7 %copy-start.4 = (f32[3072]{0:T(1024)S(1)}, f32[3072]{0:T(1024)}, u32[]{:S(2)}) copy-start(f32[3072]{0:T(1024)} %param.23) | copy-start | bytes 36868
  571.5 19.7 %copy-start.5 = (f32[3072]{0:T(1024)S(1)}, f32[3072]{0:T(1024)}, u32[]{:S(2)}) copy-start(f32[3072]{0:T(1024)} %param.24) | copy-start | bytes 36868
  571.5 19.7 %copy-start.3 = (f32[3072,4]{0,1:T(4,128)S(1)}, f32[3072,4]{0,1:T(4,128)}, u32[]{:S(2)}) copy-start(f32[3072,4]{0,1:T(4,128)} %param.20) | copy-start | bytes 147460
  571.5 155.0 %all-to-all-start.2 = ((bf16[128,4,3072]{2,1,0:T(4,128)(2,1)}), bf16[128,4,3072]{2,1,0:T(4,128)(2,1)}, u32[]{:S(2)}, u32[]{:S(2)}) async-start(bf16[128,4,3072]{2,1,0:T(4,128)(2,1)} %reshape.134), calls=%async_computation.2 | async-start | bytes 6291456 | tf_op jit(solution)/shard_map/all_to_all | solution.py:160
Sparse Core Ops, SparseCore 0:
  11.6 169.3 all-gather.9
